TPU v7x, 32 devices: a whole 2x2x4 slice. The times are simulated.
32 devices in a mesh: lat: 4 (over z), lon: 4 (over y, x), fold: 2 (over core).
Axes of the slice: x: 2, y: 2, z: 4, core: 2. Of those that a mesh axis runs over, the one named last changes fastest.
Arguments:
- field: float32 [2, 12, 640, 2560], P('fold', None, 'lat', 'lon'), may hold values from -6 to 6
- row_shift: int32 [2, 12, 640, 2560], P('fold', None, 'lat', 'lon'), may hold values from -4 to 4
- col_shift: int32 [2, 12, 640, 2560], P('fold', None, 'lat', 'lon'), may hold values from -4 to 4
- row_frac: bfloat16 [2, 12, 640, 2560], P('fold', None, 'lat', 'lon'), may hold values from 0 to 1
- col_frac: bfloat16 [2, 12, 640, 2560], P('fold', None, 'lat', 'lon'), may hold values from 0 to 1
- wave_map: int32 [16], replicated, may hold values from 0 to 1279, as said below
- legendre: float32 [16, 640, 1280], P('lon', 'lat'), may hold values from -0.25 to 0.25
- helm_coef: float32 [12], P('fold'), may hold values from 1e-06 to 0.0001
Outputs:
- spectrum: float32 [12, 4, 4, 2560], P('fold', 'lon', 'lat')
Inputs may be any that keep to these rules, and one draw needn't show every extreme that they name: `col_shift`: longitude offset of the departure cell. `wave_map`: distinct zonal wavenumbers.
All inputs are finite; a program needn't handle non-finite values.
Results may differ from a plain program's by a relative error of at most 0.0003.
Values sent between devices are 32-bit elements; how exact they have to be, the bound alone decides.
A program may use at most 64 MiB of HBM per device.

v0:
```python
import math

import jax
import jax.numpy as jnp
from jax import lax
from jax.sharding import PartitionSpec as P

SHIFT_MAX = 4


def padded_2(cells, sides, width):
    for axis, dim in sides:
        count = lax.axis_size(axis)
        head = lax.slice_in_dim(cells, 0, width, axis=dim)
        tail = lax.slice_in_dim(cells, cells.shape[dim] - width, cells.shape[dim], axis=dim)
        cells = jnp.concatenate(
            [
                lax.ppermute(tail, axis, [(i, (i + 1) % count) for i in range(count)]),
                cells,
                lax.ppermute(head, axis, [((i + 1) % count, i) for i in range(count)]),
            ],
            axis=dim,
        )
    return cells


def partner(block, axis, apart):
    count = lax.axis_size(axis)
    route = []
    for low in range(count):
        high = low | 1 << apart
        if high != low and high < count:
            route += [(low, high), (high, low)]
    return lax.ppermute(block, axis, route)


def cubic_weights(fraction):
    return (
        -fraction * (fraction - 1.0) * (fraction - 2.0) / 6.0,
        (fraction + 1.0) * (fraction - 1.0) * (fraction - 2.0) / 2.0,
        -(fraction + 1.0) * fraction * (fraction - 2.0) / 2.0,
        (fraction + 1.0) * fraction * (fraction - 1.0) / 6.0,
    )


def spread_weights(shift, weights, offset):
    placed = jnp.zeros(shift.shape, jnp.float32)
    for step in range(4):
        placed = placed + jnp.where(shift + (step - 1) == offset, weights[step], 0.0)
    return placed


def interpolate_level(items, margin):
    padded, row_shift, col_shift, row_frac, col_frac = items
    rows, cols = row_shift.shape
    offsets = list(range(1 - margin, margin + 1))
    row_weights = cubic_weights(row_frac.astype(jnp.float32))
    col_weights = cubic_weights(col_frac.astype(jnp.float32))
    col_spread = [spread_weights(col_shift, col_weights, offset) for offset in offsets]
    total = jnp.zeros((rows, cols), jnp.float32)
    for row_offset in offsets:
        band_rows = padded[margin + row_offset : margin + row_offset + rows, :]
        line = jnp.zeros((rows, cols), jnp.float32)
        for place, col_offset in enumerate(offsets):
            line = (
                line
                + col_spread[place] * band_rows[:, margin + col_offset : margin + col_offset + cols]
            )
        total = total + spread_weights(row_shift, row_weights, row_offset) * line
    return total


def interpolate(padded, row_shift, col_shift, row_frac, col_frac, margin):
    return lax.map(partial_level(margin), (padded, row_shift, col_shift, row_frac, col_frac))


def partial_level(margin):

    def apply_level(items):
        return interpolate_level(items, margin)

    return apply_level


def zonal_table(waves, first_col, count_cols, lon_total):
    col_ids = first_col + lax.iota(jnp.int32, count_cols)
    phase = col_ids[:, None] * waves[None, :] % lon_total
    angle = phase.astype(jnp.float32) * (2.0 * math.pi / lon_total)
    return jnp.stack([jnp.cos(angle), -jnp.sin(angle)], axis=1) / math.sqrt(lon_total)


def spectral_rows(source, waves, first_col, lon_total):
    table = zonal_table(waves, first_col, source.shape[2], lon_total)
    return jnp.einsum("blk,kqs->sqbl", source, table, precision=lax.Precision.HIGHEST)


def local(field, row_shift, col_shift, row_frac, col_frac, wave_map, legendre, helm_coef):
    margin = SHIFT_MAX + 2
    grid = field[0]
    levels, rows, cols = grid.shape
    half = levels // 2
    lon_total = cols * lax.axis_size("lon")
    padded = padded_2(grid, (("lat", 1), ("lon", 2)), margin)
    lat_place = lax.axis_index("lat")
    band = padded[:, rows : rows + margin, :][:, ::-1, :]
    mirrored = partner(band, "fold", 0)
    pole_rows = jnp.where(lat_place == 0, jnp.zeros_like(padded[:, :margin]), padded[:, :margin])
    after_rows = jnp.where(
        lat_place == lax.axis_size("lat") - 1, mirrored, padded[:, rows + margin :]
    )
    padded = jnp.concatenate([pole_rows, padded[:, margin : rows + margin], after_rows], axis=1)
    gridded = interpolate(padded, row_shift[0], col_shift[0], row_frac[0], col_frac[0], margin)
    hemisphere = lax.axis_index("fold") % 2
    mirror_sign = (1 - 2 * hemisphere).astype(jnp.float32)
    outgoing = lax.dynamic_slice_in_dim(gridded, (1 - hemisphere) * half, half, 0)
    incoming = partner(outgoing, "fold", 0)
    kept = lax.dynamic_slice_in_dim(gridded, hemisphere * half, half, 0)
    source = jnp.concatenate([kept + incoming, mirror_sign * (kept - incoming)], axis=0)
    lon_start = lax.axis_index("lon") * cols
    waves = wave_map
    coeffs = lax.psum_scatter(
        spectral_rows(source, waves, lon_start, lon_total), "lon", scatter_dimension=0, tiled=True
    )
    slots_here = coeffs.shape[0]
    folded = coeffs.reshape(slots_here, 2, 2, half, rows)
    degree_count = legendre.shape[2]
    slot_base = lax.axis_index("lon") * slots_here
    degrees = lax.iota(jnp.int32, degree_count)
    waves = lax.dynamic_slice_in_dim(
        wave_map, slot_base, slots_here // lax.axis_size("lat") * lax.axis_size("lat")
    )
    product = jnp.einsum("sqelk,skn->selqn", folded, legendre, precision=lax.Precision.HIGHEST)
    parity = (waves[:, None] + degrees[None, :]) % 2 == 0
    keep = (degrees[None, :] >= waves[:, None]).astype(jnp.float32)
    picked = (
        jnp.where(parity[:, None, None, :], product[:, 0], product[:, 1]) * keep[:, None, None, :]
    )
    summed = lax.psum_scatter(
        picked.reshape(
            slots_here // lax.axis_size("lat") * lax.axis_size("lat"), half, 2 * degree_count
        ),
        "lat",
        scatter_dimension=0,
        tiled=True,
    )
    degree_float = degrees.astype(jnp.float32)
    degree_pair = jnp.concatenate([degree_float, degree_float])
    damping = 1.0 + helm_coef[None, :, None] * (degree_pair * (degree_pair + 1.0))[None, None, :]
    result = summed / damping
    return jnp.transpose(result, (1, 0, 2))[:, None, :, :]


def solution(mesh):
    in_specs = (
        P("fold", None, "lat", "lon"),
        P("fold", None, "lat", "lon"),
        P("fold", None, "lat", "lon"),
        P("fold", None, "lat", "lon"),
        P("fold", None, "lat", "lon"),
        P(),
        P("lon", "lat", None),
        P("fold"),
    )
    out_specs = P("fold", "lon", "lat", None)
    return jax.shard_map(local, mesh=mesh, in_specs=in_specs, out_specs=out_specs, check_vma=False)
```

profile of v0, /device:TPU:0, one launch (start us, length us, event | category | flops | bytes accessed | tf_op | source)
XLA Modules:
  0.0 438.1 jit_solution(9955185657485921143)
XLA Ops:
  13.0 6.8 %collective-permute-done = f32[12,6,640]{2,1,0:T(8,128)S(1)} collective-permute-done((f32[12,6,640]{2,1,0:T(8,128)S(1)}, f32[12,6,640]{2,1,0:T(8,128)S(1)}, u32[]{:S(2)}, u32[]{:S(2)}) %collective-permute-start) | collective-permute-done | bytes 184352 | tf_op jit(solution)/shard_map/ppermute | solution.py:18
  46.2 5.8 %pad_maximum_fusion = f32[12,172,652]{2,1,0:T(8,128)S(1)} fusion(f32[12,172,6]{2,1,0:T(8,128)} %copy.23, f32[12,6,640]{2,1,0:T(8,128)} %copy-done.3, f32[12,160,640]{2,1,0:T(8,128)} %bitcast.475, f32[12,6,640]{2,1,0:T(8,128)S(1)} %collective-permute-done, f32[12,172,6]{2,1,0:T(8,128)} %copy.22), kind=kLoop, calls=%fused_computation.395 | loop fusion | flops 5382912 | bytes 10765824 | tf_op jit(solution)/shard_map/concatenate | solution.py:16
  57.1 262.5 %while.13 = (s32[]{:T(128)}, f32[12,160,640]{2,1,0:T(8,128)}, s32[12,160,640]{2,1,0:T(8,128)}, bf16[12,160,640]{2,1,0:T(8,128)(2,1)}, s32[12,160,640]{2,1,0:T(8,...) while((s32[]{:T(128)}, f32[12,160,640]{2,1,0:T(8,128)}, ...), condition=%wide.region_1.2_spmd, body=%wide.region_0.1_spmd.sunk | while | flops 61952012 | bytes 70636416 | solution.py:74
  57.1 4.8 %dynamic-slice_bitcast_fusion.13 = (f32[160,652]{1,0:T(8,128)S(1)}, f32[160,652]{1,0:T(8,128)S(1)}, f32[160,652]{1,0:T(8,128)S(1)}, f32[160,652]{1,0:T(8,128)S(1...) fusion(f32[12,172,652]{2,1,0:T(8,128)} %get-tuple-element.283, ...), kind=kLoop, calls=%fused_computation.37.clone.1 | loop fusion | bytes 10014772 | tf_op jit(solution)/shard_map/while/body/eval_jaxpr/slice | solution.py:62
  61.9 17.2 %fusion.209 = f32[12,160,640]{2,1,0:T(8,128)} fusion(f32[12,160,640]{2,1,0:T(8,128)} %get-tuple-element.257, s32[]{:T(128)} %get-tuple-element.256, f32[160,652]{1,0:T(8,128)S(1)} %get-tuple-element.223, f32[160,652]{1,0:T(8,128)S(1)} %get-tuple-element.224, f32[160,652]{1,0:T(8,128)S(1)} %get-tuple-element.225, ...), kind=kLoop, calls=%fused_computation.51.clone.1 | loop fusion | flops 61952000 | bytes 60621312 | tf_op jit(solution)/shard_map/while/body/jit(dynamic_update_index_in_dim)/dynamic_update_slice | solution.py:74
  83.6 17.2 %fusion.209 = f32[12,160,640]{2,1,0:T(8,128)} fusion(f32[12,160,640]{2,1,0:T(8,128)} %get-tuple-element.257, s32[]{:T(128)} %get-tuple-element.256, f32[160,652]{1,0:T(8,128)S(1)} %get-tuple-element.223, f32[160,652]{1,0:T(8,128)S(1)} %get-tuple-element.224, f32[160,652]{1,0:T(8,128)S(1)} %get-tuple-element.225, ...), kind=kLoop, calls=%fused_computation.51.clone.1 | loop fusion | flops 61952000 | bytes 60621312 | tf_op jit(solution)/shard_map/while/body/jit(dynamic_update_index_in_dim)/dynamic_update_slice | solution.py:74
  100.9 4.9 %dynamic-slice_bitcast_fusion.13 = (f32[160,652]{1,0:T(8,128)S(1)}, f32[160,652]{1,0:T(8,128)S(1)}, f32[160,652]{1,0:T(8,128)S(1)}, f32[160,652]{1,0:T(8,128)S(1...) fusion(f32[12,172,652]{2,1,0:T(8,128)} %get-tuple-element.283, ...), kind=kLoop, calls=%fused_computation.37.clone.1 | loop fusion | bytes 10014772 | tf_op jit(solution)/shard_map/while/body/eval_jaxpr/slice | solution.py:62
  105.8 17.2 %fusion.209 = f32[12,160,640]{2,1,0:T(8,128)} fusion(f32[12,160,640]{2,1,0:T(8,128)} %get-tuple-element.257, s32[]{:T(128)} %get-tuple-element.256, f32[160,652]{1,0:T(8,128)S(1)} %get-tuple-element.223, f32[160,652]{1,0:T(8,128)S(1)} %get-tuple-element.224, f32[160,652]{1,0:T(8,128)S(1)} %get-tuple-element.225, ...), kind=kLoop, calls=%fused_computation.51.clone.1 | loop fusion | flops 61952000 | bytes 60621312 | tf_op jit(solution)/shard_map/while/body/jit(dynamic_update_index_in_dim)/dynamic_update_slice | solution.py:74
  127.3 17.2 %fusion.209 = f32[12,160,640]{2,1,0:T(8,128)} fusion(f32[12,160,640]{2,1,0:T(8,128)} %get-tuple-element.257, s32[]{:T(128)} %get-tuple-element.256, f32[160,652]{1,0:T(8,128)S(1)} %get-tuple-element.223, f32[160,652]{1,0:T(8,128)S(1)} %get-tuple-element.224, f32[160,652]{1,0:T(8,128)S(1)} %get-tuple-element.225, ...), kind=kLoop, calls=%fused_computation.51.clone.1 | loop fusion | flops 61952000 | bytes 60621312 | tf_op jit(solution)/shard_map/while/body/jit(dynamic_update_index_in_dim)/dynamic_update_slice | solution.py:74
  144.5 4.9 %dynamic-slice_bitcast_fusion.13 = (f32[160,652]{1,0:T(8,128)S(1)}, f32[160,652]{1,0:T(8,128)S(1)}, f32[160,652]{1,0:T(8,128)S(1)}, f32[160,652]{1,0:T(8,128)S(1...) fusion(f32[12,172,652]{2,1,0:T(8,128)} %get-tuple-element.283, ...), kind=kLoop, calls=%fused_computation.37.clone.1 | loop fusion | bytes 10014772 | tf_op jit(solution)/shard_map/while/body/eval_jaxpr/slice | solution.py:62
  149.4 17.2 %fusion.209 = f32[12,160,640]{2,1,0:T(8,128)} fusion(f32[12,160,640]{2,1,0:T(8,128)} %get-tuple-element.257, s32[]{:T(128)} %get-tuple-element.256, f32[160,652]{1,0:T(8,128)S(1)} %get-tuple-element.223, f32[160,652]{1,0:T(8,128)S(1)} %get-tuple-element.224, f32[160,652]{1,0:T(8,128)S(1)} %get-tuple-element.225, ...), kind=kLoop, calls=%fused_computation.51.clone.1 | loop fusion | flops 61952000 | bytes 60621312 | tf_op jit(solution)/shard_map/while/body/jit(dynamic_update_index_in_dim)/dynamic_update_slice | solution.py:74
  166.7 4.8 %dynamic-slice_bitcast_fusion.13 = (f32[160,652]{1,0:T(8,128)S(1)}, f32[160,652]{1,0:T(8,128)S(1)}, f32[160,652]{1,0:T(8,128)S(1)}, f32[160,652]{1,0:T(8,128)S(1...) fusion(f32[12,172,652]{2,1,0:T(8,128)} %get-tuple-element.283, ...), kind=kLoop, calls=%fused_computation.37.clone.1 | loop fusion | bytes 10014772 | tf_op jit(solution)/shard_map/while/body/eval_jaxpr/slice | solution.py:62
  171.5 17.2 %fusion.209 = f32[12,160,640]{2,1,0:T(8,128)} fusion(f32[12,160,640]{2,1,0:T(8,128)} %get-tuple-element.257, s32[]{:T(128)} %get-tuple-element.256, f32[160,652]{1,0:T(8,128)S(1)} %get-tuple-element.223, f32[160,652]{1,0:T(8,128)S(1)} %get-tuple-element.224, f32[160,652]{1,0:T(8,128)S(1)} %get-tuple-element.225, ...), kind=kLoop, calls=%fused_computation.51.clone.1 | loop fusion | flops 61952000 | bytes 60621312 | tf_op jit(solution)/shard_map/while/body/jit(dynamic_update_index_in_dim)/dynamic_update_slice | solution.py:74
  188.7 4.6 %dynamic-slice_bitcast_fusion.13 = (f32[160,652]{1,0:T(8,128)S(1)}, f32[160,652]{1,0:T(8,128)S(1)}, f32[160,652]{1,0:T(8,128)S(1)}, f32[160,652]{1,0:T(8,128)S(1...) fusion(f32[12,172,652]{2,1,0:T(8,128)} %get-tuple-element.283, ...), kind=kLoop, calls=%fused_computation.37.clone.1 | loop fusion | bytes 10014772 | tf_op jit(solution)/shard_map/while/body/eval_jaxpr/slice | solution.py:62
  193.3 17.2 %fusion.209 = f32[12,160,640]{2,1,0:T(8,128)} fusion(f32[12,160,640]{2,1,0:T(8,128)} %get-tuple-element.257, s32[]{:T(128)} %get-tuple-element.256, f32[160,652]{1,0:T(8,128)S(1)} %get-tuple-element.223, f32[160,652]{1,0:T(8,128)S(1)} %get-tuple-element.224, f32[160,652]{1,0:T(8,128)S(1)} %get-tuple-element.225, ...), kind=kLoop, calls=%fused_computation.51.clone.1 | loop fusion | flops 61952000 | bytes 60621312 | tf_op jit(solution)/shard_map/while/body/jit(dynamic_update_index_in_dim)/dynamic_update_slice | solution.py:74
  215.0 17.2 %fusion.209 = f32[12,160,640]{2,1,0:T(8,128)} fusion(f32[12,160,640]{2,1,0:T(8,128)} %get-tuple-element.257, s32[]{:T(128)} %get-tuple-element.256, f32[160,652]{1,0:T(8,128)S(1)} %get-tuple-element.223, f32[160,652]{1,0:T(8,128)S(1)} %get-tuple-element.224, f32[160,652]{1,0:T(8,128)S(1)} %get-tuple-element.225, ...), kind=kLoop, calls=%fused_computation.51.clone.1 | loop fusion | flops 61952000 | bytes 60621312 | tf_op jit(solution)/shard_map/while/body/jit(dynamic_update_index_in_dim)/dynamic_update_slice | solution.py:74
  236.9 17.2 %fusion.209 = f32[12,160,640]{2,1,0:T(8,128)} fusion(f32[12,160,640]{2,1,0:T(8,128)} %get-tuple-element.257, s32[]{:T(128)} %get-tuple-element.256, f32[160,652]{1,0:T(8,128)S(1)} %get-tuple-element.223, f32[160,652]{1,0:T(8,128)S(1)} %get-tuple-element.224, f32[160,652]{1,0:T(8,128)S(1)} %get-tuple-element.225, ...), kind=kLoop, calls=%fused_computation.51.clone.1 | loop fusion | flops 61952000 | bytes 60621312 | tf_op jit(solution)/shard_map/while/body/jit(dynamic_update_index_in_dim)/dynamic_update_slice | solution.py:74
  258.4 17.2 %fusion.209 = f32[12,160,640]{2,1,0:T(8,128)} fusion(f32[12,160,640]{2,1,0:T(8,128)} %get-tuple-element.257, s32[]{:T(128)} %get-tuple-element.256, f32[160,652]{1,0:T(8,128)S(1)} %get-tuple-element.223, f32[160,652]{1,0:T(8,128)S(1)} %get-tuple-element.224, f32[160,652]{1,0:T(8,128)S(1)} %get-tuple-element.225, ...), kind=kLoop, calls=%fused_computation.51.clone.1 | loop fusion | flops 61952000 | bytes 60621312 | tf_op jit(solution)/shard_map/while/body/jit(dynamic_update_index_in_dim)/dynamic_update_slice | solution.py:74
  275.6 4.9 %dynamic-slice_bitcast_fusion.13 = (f32[160,652]{1,0:T(8,128)S(1)}, f32[160,652]{1,0:T(8,128)S(1)}, f32[160,652]{1,0:T(8,128)S(1)}, f32[160,652]{1,0:T(8,128)S(1...) fusion(f32[12,172,652]{2,1,0:T(8,128)} %get-tuple-element.283, ...), kind=kLoop, calls=%fused_computation.37.clone.1 | loop fusion | bytes 10014772 | tf_op jit(solution)/shard_map/while/body/eval_jaxpr/slice | solution.py:62
  280.6 17.2 %fusion.209 = f32[12,160,640]{2,1,0:T(8,128)} fusion(f32[12,160,640]{2,1,0:T(8,128)} %get-tuple-element.257, s32[]{:T(128)} %get-tuple-element.256, f32[160,652]{1,0:T(8,128)S(1)} %get-tuple-element.223, f32[160,652]{1,0:T(8,128)S(1)} %get-tuple-element.224, f32[160,652]{1,0:T(8,128)S(1)} %get-tuple-element.225, ...), kind=kLoop, calls=%fused_computation.51.clone.1 | loop fusion | flops 61952000 | bytes 60621312 | tf_op jit(solution)/shard_map/while/body/jit(dynamic_update_index_in_dim)/dynamic_update_slice | solution.py:74
  302.4 17.2 %fusion.209 = f32[12,160,640]{2,1,0:T(8,128)} fusion(f32[12,160,640]{2,1,0:T(8,128)} %get-tuple-element.257, s32[]{:T(128)} %get-tuple-element.256, f32[160,652]{1,0:T(8,128)S(1)} %get-tuple-element.223, f32[160,652]{1,0:T(8,128)S(1)} %get-tuple-element.224, f32[160,652]{1,0:T(8,128)S(1)} %get-tuple-element.225, ...), kind=kLoop, calls=%fused_computation.51.clone.1 | loop fusion | flops 61952000 | bytes 60621312 | tf_op jit(solution)/shard_map/while/body/jit(dynamic_update_index_in_dim)/dynamic_update_slice | solution.py:74
  331.0 6.3 %fusion.187 = f32[16,2,12,160]{3,0,2,1:T(8,128)} fusion(f32[6,160,640]{2,1,0:T(8,128)S(1)} %get-tuple-element.157, f32[6,160,640]{2,1,0:T(8,128)S(1)} %get-tuple-element.156, f32[640,1,16]{0,2,1:T(8,128)S(1)} %get-tuple-element.165, f32[640,1,16]{0,2,1:T(8,128)S(1)} %get-tuple-element.164), kind=kOutput, calls=%fused_computation.406 | convolution fusion | flops 473128960 | bytes 5242880 | tf_op jit(solution)/shard_map/blk,kqs->sqbl/dot_general | solution.py:94
  339.4 42.1 %all-reduce.5.cloned.1.call-done = f32[16,2,12,160]{3,0,2,1:T(8,128)} async-done(((f32[16,2,12,160]{3,0,2,1:T(8,128)}), f32[16,2,12,160]{3,0,2,1:T(8,128)}) %all-reduce.5.cloned.1.call-update) | async-done | bytes 245776
  394.1 34.8 %all-reduce.7.cloned.1.call-done = f32[4,6,2560]{2,0,1:T(4,128)} async-done(((f32[4,6,2560]{2,0,1:T(4,128)}), f32[4,6,2560]{2,0,1:T(4,128)}) %all-reduce.7.cloned.1.call-update) | async-done | bytes 245776
  (75 shorter events, 92.3 us)
Async XLA Ops:
  6.5 375.9 %copy-start = (f32[4,160,1280]{2,1,0:T(8,128)S(1)}, f32[4,160,1280]{2,1,0:T(8,128)}, u32[]{:S(2)}) copy-start(f32[4,160,1280]{2,1,0:T(8,128)} %param.16) | copy-start | bytes 9830404
  6.5 375.0 %all-reduce.5.cloned.1.call-start = ((), (), s32[]{:S(2)}) async-start(), calls=%async_computation | async-start | bytes 786432
  7.8 12.0 %collective-permute-start = (f32[12,6,640]{2,1,0:T(8,128)S(1)}, f32[12,6,640]{2,1,0:T(8,128)S(1)}, u32[]{:S(2)}, u32[]{:S(2)}) collective-permute-start(f32[12,6,640]{2,1,0:T(8,128)S(1)} %get-tuple-element.160), channel_id=1, source_target_pairs={{0,8},{8,16},{16,24},{24,0},{1,9},{9,17},{17,25},{25,1},{2,10},{10... | collective-permute-start | bytes 552968 | tf_op jit(solution)/shard_map/ppermute | solution.py:18
  10.9 12.7 %collective-permute-start.1 = (f32[12,6,640]{2,1,0:T(8,128)S(1)}, f32[12,6,640]{2,1,0:T(8,128)S(1)}, u32[]{:S(2)}, u32[]{:S(2)}) collective-permute-start(f32[12,6,640]{2,1,0:T(8,128)S(1)} %get-tuple-element.161), channel_id=1, source_target_pairs={{8,0},{16,8},{24,16},{0,24},{9,1},{17,9},{25,17},{1,25},{10,2},{18... | collective-permute-start | bytes 552968 | tf_op jit(solution)/shard_map/ppermute | solution.py:20
  23.6 3.4 copy-start.3
  29.3 5.8 %collective-permute-start.2 = (f32[12,172,6]{1,2,0:T(8,128)}, f32[12,172,6]{1,2,0:T(8,128)}, u32[]{:S(2)}, u32[]{:S(2)}) collective-permute-start(f32[12,172,6]{1,2,0:T(8,128)} %copy.20), channel_id=1, source_target_pairs={{0,2},{2,4},{4,6},{6,0},{1,3},{3,5},{5,7},{7,1},{8,10},{10,12},{12... | collective-permute-start | bytes 148616 | tf_op jit(solution)/shard_map/ppermute | solution.py:18
  33.1 4.9 %collective-permute-start.3 = (f32[12,172,6]{1,2,0:T(8,128)}, f32[12,172,6]{1,2,0:T(8,128)}, u32[]{:S(2)}, u32[]{:S(2)}) collective-permute-start(f32[12,172,6]{1,2,0:T(8,128)} %copy.21), channel_id=1, source_target_pairs={{2,0},{4,2},{6,4},{0,6},{3,1},{5,3},{7,5},{1,7},{10,8},{12,10},{14... | collective-permute-start | bytes 148616 | tf_op jit(solution)/shard_map/ppermute | solution.py:20
  46.2 6.4 %collective-permute-start.4 = (f32[12,6,652]{2,1,0:T(8,128)}, f32[12,6,652]{2,1,0:T(8,128)S(1)}, u32[]{:S(2)}, u32[]{:S(2)}) collective-permute-start(f32[12,6,652]{2,1,0:T(8,128)} %rev.3), channel_id=1, source_target_pairs={{0,1},{1,0},{2,3},{3,2},{4,5},{5,4},{6,7},{7,6},{8,9},{9,8},{10,11... | collective-permute-start | bytes 563336 | tf_op jit(solution)/shard_map/ppermute | solution.py:34
  52.0 1.2 copy-start.1
  52.0 1.6 copy-start.2
  52.0 1.6 copy-start.4
  319.6 3.8 copy-start.5
  322.9 5.1 %collective-permute-start.5 = (f32[6,160,640]{2,1,0:T(8,128)}, f32[6,160,640]{2,1,0:T(8,128)}, u32[]{:S(2)}, u32[]{:S(2)}) collective-permute-start(f32[6,160,640]{2,1,0:T(8,128)} %constant_dynamic-slice_fusion.1), channel_id=1, source_target_pairs={{0,1},{1,0},{2,3},{3,2},{4,5},{5,4},{6,7},{7,6},{8,9},{9,8},{10,11... | collective-permute-start | bytes 7372808 | tf_op jit(solution)/shard_map/ppermute | solution.py:34
  330.9 7.3 %copy-start.8 = (u32[32]{0:T(128)S(1)}, u32[32]{0:T(128)}, u32[]{:S(2)}) copy-start(u32[32]{0:T(128)} %constant.212) | copy-start | bytes 388
  337.3 91.5 %all-reduce.7.cloned.1.call-start = ((), (), s32[]{:S(2)}) async-start(), calls=%async_computation.1 | async-start | bytes 491520
  384.4 9.0 %copy-start.7 = (u32[32]{0:T(128)S(1)}, u32[32]{0:T(128)}, u32[]{:S(2)}) copy-start(u32[32]{0:T(128)} %constant.216) | copy-start | bytes 388
  384.4 44.5 %copy-start.6 = (f32[6]{0:T(128)S(1)}, f32[6]{0:T(128)}, u32[]{:S(2)}) copy-start(f32[6]{0:T(128)} %param.17) | copy-start | bytes 76
Sparse Core Ops, SparseCore 0:
  337.4 44.0 all-reduce.4
  393.5 35.2 all-reduce.6
where the time goes:
time: 439 us; the launch traced here: 438 us
  other arithmetic  229 us (52%)
  waiting for transfers between devices  92.8 us (21%)
  local copies, waits for them, and re-layouts  85 us (19%)
  between operations  14.2 us (3%)
  starting transfers between devices  8.85 us (2%)
  matrix products  8.24 us (2%)
    dynamic_update_slice x12, other arithmetic, interpolate(): lax.map(partial_level(margin), (padded, row_shift, col_shift, row_frac, c...  207 us
    unnamed x4, waiting for transfers between devices  76.9 us
    slice x12, local copies, waits for them, and re-layouts, interpolate_level(): band_rows = padded[margin + row_offset:margin + row_offset + rows, :]  55.6 us
  transfers between devices with their start and end apart: 8, of which 7 were waited for; matrix products, arithmetic and copies ran while one was open for 3% of the time, Pallas kernels for 0%

commit v1 on v0

v1 whole, which is shorter than its diff:
```python
import functools
import math

import jax
import jax.numpy as jnp
from jax import lax
from jax.experimental import pallas as pl
from jax.experimental.pallas import tpu as pltpu
from jax.sharding import PartitionSpec as P

SHIFT_MAX = 4
LANES = 128
HEAD = 8


def cubic_weights(t):
    tm, tp, td = t - 1.0, t + 1.0, t - 2.0
    outer = t * tm
    inner = tp * td
    return (
        outer * (td * (-1.0 / 6.0)),
        inner * (tm * 0.5),
        inner * (t * -0.5),
        outer * (tp * (1.0 / 6.0)),
    )


def tiles_of(cols, margin):
    usable = LANES - 2 * margin + 1
    count = -(-cols // usable)
    stride = -(-cols // count)
    tiles = []
    for t in range(count):
        low, high = t * stride, min(cols, (t + 1) * stride)
        start = min(low, cols - LANES)
        base = margin - 1 if start == low else -margin
        tiles.append((start, base, low, high))
    return tiles


def interp_kernel(
    tiles,
    margin,
    field,
    north,
    south,
    west,
    east,
    row_shift,
    col_shift,
    row_frac,
    col_frac,
    table,
    out,
    source,
    row_t,
    col_t,
    grid,
):
    rows, cols = field.shape[1:]
    row_t[...] = row_frac[0].astype(jnp.float32)
    col_t[...] = col_frac[0].astype(jnp.float32)
    for t, (start, base, _, _) in enumerate(tiles):
        first = start - base
        lead = max(0, -first)
        trail = max(0, first + LANES - cols)
        mid_a, mid_b = first + lead, first + LANES - trail
        a, b = lead, LANES - trail
        source[t, HEAD - margin : HEAD, a:b] = north[0, :, mid_a:mid_b]
        source[t, HEAD : HEAD + rows, a:b] = field[0, :, mid_a:mid_b]
        source[t, HEAD + rows : HEAD + rows + margin, a:b] = south[0, :, mid_a:mid_b]
        span = rows + 2 * margin
        if lead:
            source[t, HEAD - margin : HEAD - margin + span, 0:lead] = west[0, :, margin - lead :]
        if trail:
            source[t, HEAD - margin : HEAD - margin + span, b:LANES] = east[0, :, :trail]

    lane = lax.broadcasted_iota(jnp.int32, (8, LANES), 1)
    blocks = rows // 8
    unroll = next(u for u in (5, 4, 3, 2, 1) if blocks % u == 0)
    window = range(1 - margin, margin + 1)

    for t, (start, base, _, _) in enumerate(tiles):
        low = -base + (margin - 1)
        high = LANES - 1 - base - margin
        place = jnp.clip(lane, low, high) + (base - 1)
        floor, shift = start // LANES * LANES, start % LANES

        def read(ref, at):
            if shift == 0:
                return ref[at, floor : floor + LANES]
            pair = ref[at, floor : floor + 2 * LANES]
            return pltpu.roll(pair, 2 * LANES - shift, 1)[:, :LANES]

        def one(j):
            at = pl.ds(pl.multiple_of(8 * j, 8), 8)
            cs = read(col_shift.at[0], at)
            rs = read(row_shift.at[0], at)
            wc = cubic_weights(read(col_t, at))
            wr = cubic_weights(read(row_t, at))
            origin = place + cs
            index = [origin + step for step in range(4)]
            lines = []
            for offset in window:
                cells = source[t, pl.ds(8 * j + (HEAD + offset), 8), :]
                line = None
                for step in range(4):
                    taken = jnp.take_along_axis(
                        cells, index[step], axis=1, mode="promise_in_bounds"
                    )
                    term = wc[step] * taken
                    line = term if line is None else line + term
                lines.append(line)
            left = rs + SHIFT_MAX
            reach = SHIFT_MAX
            while reach >= 1:
                far = left >= reach + (1 if reach > 1 else 0)
                count = len(lines) - reach
                lines = [jnp.where(far, lines[i + reach], lines[i]) for i in range(count)]
                left = jnp.where(far, left - reach, left)
                if reach == 1:
                    break
                reach //= 2
            far = left >= 1
            if len(lines) > 4:
                lines = [jnp.where(far, lines[i + 1], lines[i]) for i in range(4)]
            total = wr[0] * lines[0]
            for step in range(1, 4):
                total = total + wr[step] * lines[step]
            grid[at, t * LANES : (t + 1) * LANES] = total

        def body(outer, carry):
            for k in range(unroll):
                one(outer * unroll + k)
            return carry

        lax.fori_loop(0, blocks // unroll, body, 0)

    half = table.shape[1] // 2
    values = grid[...]
    top = values.astype(jnp.bfloat16)
    rest = (values - top.astype(jnp.float32)).astype(jnp.bfloat16)
    both = jnp.dot(top, table[...], preferred_element_type=jnp.float32)
    more = jnp.dot(rest, table[:, :half], preferred_element_type=jnp.float32)
    out[0] = (both[:, :half] + both[:, half:] + more).T


def interpolated_waves(field, halos, shifts, fracs, table, tiles, margin):
    levels, rows, cols = field.shape
    north, south, west, east = halos

    def whole(x):
        return pl.BlockSpec((1,) + x.shape[1:], lambda i: (i, 0, 0))

    operands = [field, north, south, west, east, *shifts, *fracs]
    half = table.shape[1] // 2
    return pl.pallas_call(
        functools.partial(interp_kernel, tiles, margin),
        grid=(levels,),
        in_specs=[whole(x) for x in operands]
        + [pl.BlockSpec(table.shape, lambda i: (0, 0))],
        out_specs=pl.BlockSpec((1, half, rows), lambda i: (i, 0, 0)),
        out_shape=jax.ShapeDtypeStruct((levels, half, rows), jnp.float32),
        scratch_shapes=[
            pltpu.VMEM((len(tiles), rows + 16, LANES), jnp.float32),
            pltpu.VMEM((rows, cols), jnp.float32),
            pltpu.VMEM((rows, cols), jnp.float32),
            pltpu.VMEM((rows, len(tiles) * LANES), jnp.float32),
        ],
    )(*operands, table)


def zonal_table(waves, first_col, tiles, lon_total):
    lane = lax.broadcasted_iota(jnp.int32, (len(tiles), LANES), 1)
    starts = jnp.array([t[0] for t in tiles], jnp.int32)[:, None]
    lows = jnp.array([t[2] for t in tiles], jnp.int32)[:, None]
    highs = jnp.array([t[3] for t in tiles], jnp.int32)[:, None]
    local_col = lane + starts
    own = ((local_col >= lows) & (local_col < highs)).reshape(-1)
    col = (first_col + local_col).reshape(-1)
    phase = waves[:, None] * col[None, :] % lon_total
    angle = phase.astype(jnp.float32) * (2.0 * math.pi / lon_total)
    pair = jnp.stack([jnp.cos(angle), -jnp.sin(angle)], axis=1) / math.sqrt(lon_total)
    pair = jnp.where(own, pair, 0.0)
    full = pair.reshape(-1, pair.shape[-1])
    top = full.astype(jnp.bfloat16)
    rest = (full - lax.reduce_precision(full, 8, 7)).astype(jnp.bfloat16)
    return jnp.concatenate([top, rest], axis=0).T


def halos_of(grid, margin):
    rows, cols = grid.shape[1:]
    n_lat, n_fold, n_lon = (lax.axis_size(a) for a in ("lat", "fold", "lon"))
    place = lax.axis_index("lat")
    head, tail = grid[:, :margin], grid[:, rows - margin :]
    north = lax.ppermute(tail, "lat", [(i, i + 1) for i in range(n_lat - 1)])
    below = lax.ppermute(head, "lat", [(i + 1, i) for i in range(n_lat - 1)])
    last = n_lat - 1
    mirror = lax.ppermute(
        tail[:, ::-1],
        ("lat", "fold"),
        [(last * n_fold + f, last * n_fold + (f ^ 1)) for f in range(n_fold)],
    )
    south = jnp.where(place == last, mirror, below)

    def edge(a, b):
        return jnp.concatenate([north[:, :, a:b], grid[:, :, a:b], south[:, :, a:b]], axis=1)

    west = lax.ppermute(
        edge(cols - margin, cols), "lon", [(i, (i + 1) % n_lon) for i in range(n_lon)]
    )
    east = lax.ppermute(edge(0, margin), "lon", [((i + 1) % n_lon, i) for i in range(n_lon)])
    return north, south, west, east


def local(field, row_shift, col_shift, row_frac, col_frac, wave_map, legendre, helm_coef):
    margin = SHIFT_MAX + 2
    grid = field[0]
    levels, rows, cols = grid.shape
    half = levels // 2
    n_lon, n_lat, n_fold = (lax.axis_size(a) for a in ("lon", "lat", "fold"))
    lon_total = cols * n_lon
    lon_place = lax.axis_index("lon")
    tiles = tiles_of(cols, margin)
    table = zonal_table(wave_map, lon_place * cols, tiles, lon_total)
    waves_here = interpolated_waves(
        grid,
        halos_of(grid, margin),
        (row_shift[0], col_shift[0]),
        (row_frac[0], col_frac[0]),
        table,
        tiles,
        margin,
    )
    slots = wave_map.shape[0]
    slots_here = slots // n_lon
    hemisphere = lax.axis_index("fold") % 2
    sign = (1 - 2 * hemisphere).astype(jnp.float32)
    by_slot = jnp.transpose(waves_here.reshape(levels, slots, 2, rows), (1, 2, 0, 3))
    coeffs = lax.psum_scatter(by_slot, "lon", scatter_dimension=0, tiled=True)
    outgoing = lax.dynamic_slice_in_dim(coeffs, (1 - hemisphere) * half, half, 2)
    incoming = lax.ppermute(outgoing, "fold", [(f, f ^ 1) for f in range(n_fold)])
    kept = lax.dynamic_slice_in_dim(coeffs, hemisphere * half, half, 2)
    folded = jnp.stack([kept + incoming, sign * (kept - incoming)], axis=2)
    degree_count = legendre.shape[2]
    degrees = lax.iota(jnp.int32, degree_count)
    waves = lax.dynamic_slice_in_dim(wave_map, lon_place * slots_here, slots_here)
    product = jnp.einsum("sqelk,skn->selqn", folded, legendre, precision=lax.Precision.HIGHEST)
    parity = (waves[:, None] + degrees[None, :]) % 2 == 0
    keep = degrees[None, :] >= waves[:, None]
    picked = jnp.where(parity[:, None, None, :], product[:, 0], product[:, 1])
    picked = jnp.where(keep[:, None, None, :], picked, 0.0)
    summed = lax.psum_scatter(
        picked.reshape(slots_here, half, 2 * degree_count), "lat", scatter_dimension=0, tiled=True
    )
    degree_float = degrees.astype(jnp.float32)
    pair = jnp.concatenate([degree_float, degree_float])
    damping = 1.0 + helm_coef[None, :, None] * (pair * (pair + 1.0))[None, None, :]
    return jnp.transpose(summed / damping, (1, 0, 2))[:, None, :, :]


def solution(mesh):
    block = P("fold", None, "lat", "lon")
    in_specs = (block,) * 5 + (P(), P("lon", "lat", None), P("fold"))
    out_specs = P("fold", "lon", "lat", None)
    return jax.shard_map(local, mesh=mesh, in_specs=in_specs, out_specs=out_specs, check_vma=False)
```

time: 439 us -> 421 us (0.959)
  Pallas kernels: 0 us -> 276 us
  other arithmetic: 229 us -> 14.8 us
  local copies, waits for them, and re-layouts: 85 us -> 37.2 us
  waiting for transfers between devices: 92.8 us -> 64.8 us
  matrix products: 8.24 us -> 1.92 us
    pallas_call x0 -> x1, Pallas kernels: none -> 276 us  [interpolated_waves(): pl.pallas_call(functools.partial(interp_kernel, tiles, margin), grid=(lev...]
    dynamic_update_slice x12 -> x0, other arithmetic: 207 us -> none  [interpolate(): lax.map(partial_level(margin), (padded, row_shift, col_shift, row_frac, c...]
    slice x19 -> x13, local copies, waits for them, and re-layouts: 65.5 us -> 21.6 us  [the longest x3 7.72 us: edge(): grid[:, :, a:b]]
    unnamed x4 -> x3, waiting for transfers between devices: 76.9 us -> 34.8 us
    reduce_scatter x0 -> x1, waiting for transfers between devices: none -> 27 us  [local(): coeffs = lax.psum_scatter(by_slot, 'lon', scatter_dimension=0, tiled=True)]
    ppermute x6, waiting for transfers between devices: 16 us -> 3 us  [the longest x1 1.86 us: halos_of(): lax.ppermute(edge(0, margin), 'lon', [((i + 1) % n_lon, i) for i in range...]
    concatenate x2, other arithmetic: 9.07 us -> 2.68 us  [edge(): jnp.concatenate([north[:, :, a:b], grid[:, :, a:b], south[:, :, a:b]], ax...]
    dot_general x1 -> x0, matrix products: 6.34 us -> none  [spectral_rows(): jnp.einsum('blk,kqs->sqbl', source, table, precision=lax.Precision.HIGHEST)]
  transfers between devices with their start and end apart: 8 -> 8, of which waited for: 7 -> 4; matrix products, arithmetic and copies ran while one was open for 3% -> 6% of each run, Pallas kernels for 0% -> 0%
where the time goes in v1:
time: 421 us; the launch traced here: 420 us
  Pallas kernels  276 us (66%)
  waiting for transfers between devices  64.8 us (15%)
  local copies, waits for them, and re-layouts  37.2 us (9%)
  other arithmetic  14.8 us (4%)
  between operations  13.6 us (3%)
  starting transfers between devices  11.4 us (3%)
    pallas_call x1, Pallas kernels, interpolated_waves(): pl.pallas_call(functools.partial(interp_kernel, tiles, margin), grid=(lev...  276 us
    unnamed x3, waiting for transfers between devices  34.8 us
    reduce_scatter x1, waiting for transfers between devices, local(): coeffs = lax.psum_scatter(by_slot, 'lon', scatter_dimension=0, tiled=True)  27 us
  transfers between devices with their start and end apart: 8, of which 4 were waited for; matrix products, arithmetic and copies ran while one was open for 6% of the time, Pallas kernels for 0%

profile of v1, /device:TPU:0, one launch (start us, length us, event | category | flops | bytes accessed | tf_op | source)
XLA Modules:
  0.0 420.0 jit_solution(14501469153957376521)
XLA Ops:
  6.5 2.0 fusion.24
  8.6 5.7 %collective-permute-start = (f32[12,6,640]{2,1,0:T(8,128)}, f32[12,6,640]{2,1,0:T(8,128)}, u32[]{:S(2)}, u32[]{:S(2)}) collective-permute-start(f32[12,6,640]{2,1,0:T(8,128)} %get-tuple-element.8), channel_id=1, source_target_pairs={{0,8},{8,16},{16,24},{1,9},{9,17},{17,25},{2,10},{10,18},{18,26},{... | collective-permute-start | bytes 552968 | tf_op jit(solution)/shard_map/ppermute | solution.py:196
  14.2 3.1 rev.3
  20.1 3.1 fusion.23
  24.6 2.3 copy.38
  26.9 2.3 copy.35
  29.3 1.9 fusion.5
  31.2 1.8 select_convert_fusion
  34.7 1.6 copy.39
  36.3 1.6 copy.36
  42.5 1.7 pad_maximum_fusion
  48.1 1.8 maximum_bitcast_fusion.table
  50.0 1.9 collective-permute-done.4
  51.8 2.3 copy.43.east
  54.1 2.3 copy.42.west
  56.4 276.4 %shard_map.109 = f32[12,32,160]{2,1,0:T(8,128)} custom-call(f32[12,160,640]{2,1,0:T(8,128)} %bitcast.42, f32[12,6,640]{2,1,0:T(8,128)} %collective-permute-done.north, f32[12,6,640]{2,1,0:T(8,128)} %copy-done.1, f32[12,172,6]{2,1,0:T(8,128)} %copy.42.west, f32[12,172,6]{2,1,0:T(8,128)} %copy.43.east, s32[12,160,640]{2,1,0:T(8,128)} %bitcast.43, ...), custom_call_target="tpu_custom_call" | custom-call | tf_op jit(solution)/shard_map/pallas_call | solution.py:157
  332.8 2.0 copy.50
  335.0 27.0 %reduce-scatter.3.cloned.1.call-done = f32[4,2,12,160]{3,2,1,0:T(8,128)} async-done(((f32[16,2,12,160]{3,2,1,0:T(8,128)}), f32[4,2,12,160]{3,2,1,0:T(8,128)}) %reduce-scatter.3.cloned.1.call-update) | async-done | bytes 61456 | tf_op jit(solution)/shard_map/reduce_scatter | solution.py:240
  365.2 1.9 fusion.2
  369.9 1.8 copy.46
  371.7 1.9 squeeze.26
  373.6 1.7 select_select_fusion
  376.0 34.8 %all-reduce.3.cloned.1.call-done = f32[4,6,2560]{2,0,1:T(4,128)} async-done(((f32[4,6,2560]{2,0,1:T(4,128)}), f32[4,6,2560]{2,0,1:T(4,128)}) %all-reduce.3.cloned.1.call-update) | async-done | bytes 245776
  410.8 2.4 fusion.9
  (54 shorter events, 21.3 us)
Async XLA Ops:
  6.5 358.6 %copy-start = (f32[4,160,1280]{2,1,0:T(8,128)S(1)}, f32[4,160,1280]{2,1,0:T(8,128)}, u32[]{:S(2)}) copy-start(f32[4,160,1280]{2,1,0:T(8,128)} %param.17) | copy-start | bytes 9830404
  6.5 16.6 %copy-start.2 = (s32[6]{0:T(128)S(1)}, s32[6]{0:T(128)}, u32[]{:S(2)}) copy-start(s32[6]{0:T(128)} %constant.75.clone) | copy-start | bytes 76
  6.5 16.7 %copy-start.3 = (s32[16]{0:T(128)S(1)}, s32[16]{0:T(128)}, u32[]{:S(2)}) copy-start(s32[16]{0:T(128)} %param.16) | copy-start | bytes 196
  6.5 355.4 %reduce-scatter.3.cloned.1.call-start = ((), (), s32[]{:S(2)}) async-start(), calls=%async_computation.1 | async-start | bytes 655360 | tf_op jit(solution)/shard_map/reduce_scatter | solution.py:240
  8.6 29.3 %collective-permute-start = (f32[12,6,640]{2,1,0:T(8,128)}, f32[12,6,640]{2,1,0:T(8,128)}, u32[]{:S(2)}, u32[]{:S(2)}) collective-permute-start(f32[12,6,640]{2,1,0:T(8,128)} %get-tuple-element.8), channel_id=1, source_target_pairs={{0,8},{8,16},{16,24},{1,9},{9,17},{17,25},{2,10},{10,18},{18,26},{... | collective-permute-start | bytes 552968 | tf_op jit(solution)/shard_map/ppermute | solution.py:196
  17.4 15.6 %collective-permute-start.1 = (f32[12,6,640]{2,1,0:T(8,128)}, f32[12,6,640]{2,1,0:T(8,128)}, u32[]{:S(2)}, u32[]{:S(2)}) collective-permute-start(f32[12,6,640]{2,1,0:T(8,128)} %rev.3), channel_id=1, source_target_pairs={{24,25},{25,24},{26,27},{27,26},{28,29},{29,28},{30,31},{31,30}} | collective-permute-start | bytes 552968 | tf_op jit(solution)/shard_map/ppermute | solution.py:199
  18.8 14.3 %collective-permute-start.2 = (f32[12,6,640]{2,1,0:T(8,128)}, f32[12,6,640]{2,1,0:T(8,128)}, u32[]{:S(2)}, u32[]{:S(2)}) collective-permute-start(f32[12,6,640]{2,1,0:T(8,128)} %get-tuple-element.7), channel_id=1, source_target_pairs={{8,0},{16,8},{24,16},{9,1},{17,9},{25,17},{10,2},{18,10},{26,18},{... | collective-permute-start | bytes 552968 | tf_op jit(solution)/shard_map/ppermute | solution.py:197
  20.1 9.2 %copy-start.5 = (s32[6]{0:T(128)S(1)}, s32[6]{0:T(128)}, u32[]{:S(2)}) copy-start(s32[6]{0:T(128)} %constant.77.clone) | copy-start | bytes 76
  34.0 22.4 %copy-start.1 = (f32[12,6,640]{2,1,0:T(8,128)}, f32[12,6,640]{2,1,0:T(8,128)S(1)}, u32[]{:S(2)}) copy-start(f32[12,6,640]{2,1,0:T(8,128)S(1)} %broadcast_select_fusion.south) | copy-start | bytes 552964
  44.1 10.0 %collective-permute-start.3 = (f32[12,172,6]{1,2,0:T(8,128)}, f32[12,172,6]{1,2,0:T(8,128)}, u32[]{:S(2)}, u32[]{:S(2)}) collective-permute-start(f32[12,172,6]{1,2,0:T(8,128)} %pad_maximum_fusion), channel_id=1, source_target_pairs={{0,2},{2,4},{4,6},{6,0},{1,3},{3,5},{5,7},{7,1},{8,10},{10,12},{12... | collective-permute-start | bytes 148616 | tf_op jit(solution)/shard_map/ppermute | solution.py:209
  46.6 5.2 %collective-permute-start.4 = (f32[12,172,6]{1,2,0:T(8,128)S(1)}, f32[12,172,6]{1,2,0:T(8,128)}, u32[]{:S(2)}, u32[]{:S(2)}) collective-permute-start(f32[12,172,6]{1,2,0:T(8,128)S(1)} %pad_maximum_fusion.1), channel_id=1, source_target_pairs={{2,0},{4,2},{6,4},{0,6},{3,1},{5,3},{7,5},{1,7},{10,8},{12,10},{14... | collective-permute-start | bytes 148616 | tf_op jit(solution)/shard_map/ppermute | solution.py:212
  334.9 75.9 %all-reduce.3.cloned.1.call-start = ((), (), s32[]{:S(2)}) async-start(), calls=%async_computation.2 | async-start | bytes 491520
  362.9 1.3 collective-permute-start.5
  365.2 10.2 %copy-start.6 = (u32[32]{0:T(128)S(1)}, u32[32]{0:T(128)}, u32[]{:S(2)}) copy-start(u32[32]{0:T(128)} %constant.85) | copy-start | bytes 388
  367.1 43.7 %copy-start.4 = (f32[6]{0:T(128)S(1)}, f32[6]{0:T(128)}, u32[]{:S(2)}) copy-start(f32[6]{0:T(128)} %param.18) | copy-start | bytes 76
Sparse Core Ops, SparseCore 0:
  335.0 26.9 reduce-scatter.2
  375.5 35.2 all-reduce.2

commit v2 on v1

v2 whole, which is shorter than its diff:
```python
import functools
import math

import jax
import jax.numpy as jnp
from jax import lax
from jax.experimental import pallas as pl
from jax.experimental.pallas import tpu as pltpu
from jax.sharding import PartitionSpec as P

SHIFT_MAX = 4
LANES = 128
HEAD = 8


def cubic_weights(t):
    tm, tp, td = t - 1.0, t + 1.0, t - 2.0
    outer = t * tm
    inner = tp * td
    return (
        outer * (td * (-1.0 / 6.0)),
        inner * (tm * 0.5),
        inner * (t * -0.5),
        outer * (tp * (1.0 / 6.0)),
    )


def interp_kernel(
    margin,
    last,
    field,
    north,
    below,
    mirror,
    west,
    east,
    row_shift,
    col_shift,
    row_frac,
    col_frac,
    table,
    out,
    padded,
    source,
    row_t,
    col_t,
    grid,
):
    rows, cols = field.shape[1:]
    count = cols // LANES
    span = rows + 2 * HEAD
    row_t[...] = row_frac[0].astype(jnp.float32)
    col_t[...] = col_frac[0].astype(jnp.float32)
    inner = slice(LANES, LANES + cols)
    padded[0:HEAD, inner] = north[0]
    padded[HEAD : HEAD + rows, inner] = field[0]
    at_last = jnp.full((1, cols), last[0], jnp.int32) == 1
    for i in range(HEAD):
        line = jnp.where(at_last, mirror[0, HEAD - 1 - i : HEAD - i], below[0, i : i + 1])
        padded[HEAD + rows + i : HEAD + rows + i + 1, inner] = line
    padded[:, LANES - HEAD : LANES] = west[0].T
    padded[:, LANES + cols : LANES + cols + HEAD] = east[0].T

    lane = lax.broadcasted_iota(jnp.int32, (span, LANES), 1)
    for c in range(2 * margin):
        move = c + 1 - margin
        side = (move > 0) - (move < 0)
        near = [
            padded[:, (t + 1) * LANES : (t + 2) * LANES]
            for t in range(min(0, side), count + max(0, side))
        ]
        if side:
            near = [pltpu.roll(x, -move % LANES, 1) for x in near]
        for t in range(count):
            if side > 0:
                source[c, t] = jnp.where(lane < LANES - move, near[t], near[t + 1])
            elif side < 0:
                source[c, t] = jnp.where(lane >= -move, near[t + 1], near[t])
            else:
                source[c, t] = near[t]

    blocks = rows // 8
    unroll = next(u for u in (2, 1) if blocks % u == 0)
    window = range(1 - margin, margin + 1)

    for t in range(count):

        def read(ref, at):
            return ref[at, t * LANES : (t + 1) * LANES]

        def one(j):
            at = pl.ds(pl.multiple_of(8 * j, 8), 8)
            cs = read(col_shift.at[0], at)
            rs = read(row_shift.at[0], at)
            wc = cubic_weights(read(col_t, at))
            wr = cubic_weights(read(row_t, at))
            lines = [None] * len(window)
            hits = [cs == v for v in range(-SHIFT_MAX, SHIFT_MAX + 1)]
            spread = []
            for place_at in range(len(window)):
                w = None
                for step in range(4):
                    v = place_at - step
                    if 0 <= v < len(hits):
                        w = jnp.where(hits[v], wc[step], 0.0 if w is None else w)
                spread.append(w)
            for slot, offset in enumerate(window):
                for c in range(len(window)):
                    cells = source[c, t, pl.ds(8 * j + (HEAD + offset), 8), :]
                    term = spread[c] * cells
                    lines[slot] = term if c == 0 else lines[slot] + term
            left = rs + SHIFT_MAX
            reach = SHIFT_MAX
            while reach >= 1:
                far = left >= reach + (1 if reach > 1 else 0)
                taps = len(lines) - reach
                lines = [jnp.where(far, lines[i + reach], lines[i]) for i in range(taps)]
                left = jnp.where(far, left - reach, left)
                if reach == 1:
                    break
                reach //= 2
            far = left >= 1
            if len(lines) > 4:
                lines = [jnp.where(far, lines[i + 1], lines[i]) for i in range(4)]
            total = wr[0] * lines[0]
            for step in range(1, 4):
                total = total + wr[step] * lines[step]
            grid[at, t * LANES : (t + 1) * LANES] = total

        def body(outer, carry):
            for k in range(unroll):
                one(outer * unroll + k)
            return carry

        lax.fori_loop(0, blocks // unroll, body, 0)

    half = table.shape[1] // 2
    values = grid[...]
    top = values.astype(jnp.bfloat16)
    rest = (values - top.astype(jnp.float32)).astype(jnp.bfloat16)
    both = jnp.dot(top, table[...], preferred_element_type=jnp.float32)
    more = jnp.dot(rest, table[:, :half], preferred_element_type=jnp.float32)
    sums = both[:, :half] + both[:, half:] + more
    out[0] = sums.T.reshape(out.shape[1:])


def interpolated_waves(field, halos, shifts, fracs, table, last, n_lon, margin):
    levels, rows, cols = field.shape

    def whole(x):
        return pl.BlockSpec((1,) + x.shape[1:], lambda i: (i, 0, 0))

    operands = [field, *halos, *shifts, *fracs]
    shape = (levels, n_lon, table.shape[1] // 2 // n_lon, rows)
    return pl.pallas_call(
        functools.partial(interp_kernel, margin),
        grid=(levels,),
        in_specs=[pl.BlockSpec(memory_space=pltpu.SMEM)]
        + [whole(x) for x in operands]
        + [pl.BlockSpec(table.shape, lambda i: (0, 0))],
        out_specs=pl.BlockSpec((1,) + shape[1:], lambda i: (i, 0, 0, 0)),
        out_shape=jax.ShapeDtypeStruct(shape, jnp.float32),
        scratch_shapes=[
            pltpu.VMEM((rows + 2 * HEAD, cols + 2 * LANES), jnp.float32),
            pltpu.VMEM((2 * margin, cols // LANES, rows + 2 * HEAD, LANES), jnp.float32),
            pltpu.VMEM((rows, cols), jnp.float32),
            pltpu.VMEM((rows, cols), jnp.float32),
            pltpu.VMEM((rows, cols), jnp.float32),
        ],
    )(last, *operands, table)


def zonal_table(waves, first_col, cols, lon_total):
    col = first_col + lax.iota(jnp.int32, cols)
    phase = waves[:, None] * col[None, :] % lon_total
    angle = phase.astype(jnp.float32) * (2.0 * math.pi / lon_total)
    pair = jnp.stack([jnp.cos(angle), -jnp.sin(angle)], axis=1) / math.sqrt(lon_total)
    full = pair.reshape(-1, cols)
    top = full.astype(jnp.bfloat16)
    rest = (full - lax.reduce_precision(full, 8, 7)).astype(jnp.bfloat16)
    return jnp.concatenate([top, rest], axis=0).T


def halos_of(grid):
    rows, cols = grid.shape[1:]
    n_lat, n_fold, n_lon = (lax.axis_size(a) for a in ("lat", "fold", "lon"))
    last = n_lat - 1
    at_last = lax.axis_index("lat") == last
    head, tail = grid[:, :HEAD], grid[:, rows - HEAD :]
    north = lax.ppermute(tail, "lat", [(i, i + 1) for i in range(last)])
    below = lax.ppermute(head, "lat", [(i + 1, i) for i in range(last)])
    route = [(last * n_fold + f, last * n_fold + (f ^ 1)) for f in range(n_fold)]
    mirror = lax.ppermute(tail, ("lat", "fold"), route)

    def edge(a, b):
        south = jnp.where(at_last, mirror[:, ::-1, a:b], below[:, :, a:b])
        strip = jnp.concatenate([north[:, :, a:b], grid[:, :, a:b], south], axis=1)
        return jnp.swapaxes(strip, 1, 2)

    ring = [(i, (i + 1) % n_lon) for i in range(n_lon)]
    west = lax.ppermute(edge(cols - HEAD, cols), "lon", ring)
    east = lax.ppermute(edge(0, HEAD), "lon", [(b, a) for a, b in ring])
    return at_last.astype(jnp.int32).reshape(1), (north, below, mirror, west, east)


def scatter_sum(pieces, axis):
    count = lax.axis_size(axis)
    place = lax.axis_index(axis)
    total = lax.dynamic_index_in_dim(pieces, place, 0, keepdims=False)
    arrived = []
    for step in range(1, count):
        piece = lax.dynamic_index_in_dim(pieces, (place + step) % count, 0, keepdims=False)
        arrived.append(lax.ppermute(piece, axis, [(i, (i + step) % count) for i in range(count)]))
    for part in arrived:
        total = total + part
    return total


def local(field, row_shift, col_shift, row_frac, col_frac, wave_map, legendre, helm_coef):
    margin = SHIFT_MAX + 2
    grid = field[0]
    levels, rows, cols = grid.shape
    half = levels // 2
    n_lon, n_lat, n_fold = (lax.axis_size(a) for a in ("lon", "lat", "fold"))
    lon_place = lax.axis_index("lon")
    table = zonal_table(wave_map, lon_place * cols, cols, cols * n_lon)
    last, halos = halos_of(grid)
    waves_here = interpolated_waves(
        grid,
        halos,
        (row_shift[0], col_shift[0]),
        (row_frac[0], col_frac[0]),
        table,
        last,
        n_lon,
        margin,
    )
    slots_here = wave_map.shape[0] // n_lon
    hemisphere = lax.axis_index("fold") % 2
    sign = (1 - 2 * hemisphere).astype(jnp.float32)
    coeffs = scatter_sum(jnp.swapaxes(waves_here, 0, 1), "lon")
    outgoing = lax.dynamic_slice_in_dim(coeffs, (1 - hemisphere) * half, half, 0)
    incoming = lax.ppermute(outgoing, "fold", [(f, f ^ 1) for f in range(n_fold)])
    kept = lax.dynamic_slice_in_dim(coeffs, hemisphere * half, half, 0)
    folded = jnp.stack([kept + incoming, sign * (kept - incoming)], axis=0)
    folded = jnp.transpose(folded.reshape(2, half, slots_here, 2, rows), (2, 3, 0, 1, 4))
    degree_count = legendre.shape[2]
    degrees = lax.iota(jnp.int32, degree_count)
    waves = lax.dynamic_slice_in_dim(wave_map, lon_place * slots_here, slots_here)
    product = jnp.einsum("sqelk,skn->selqn", folded, legendre, precision=lax.Precision.HIGHEST)
    parity = (waves[:, None] + degrees[None, :]) % 2 == 0
    keep = degrees[None, :] >= waves[:, None]
    picked = jnp.where(parity[:, None, None, :], product[:, 0], product[:, 1])
    picked = jnp.where(keep[:, None, None, :], picked, 0.0)
    summed = scatter_sum(
        picked.reshape(n_lat, slots_here // n_lat, half, 2 * degree_count), "lat"
    )
    degree_float = degrees.astype(jnp.float32)
    pair = jnp.concatenate([degree_float, degree_float])
    damping = 1.0 + helm_coef[None, :, None] * (pair * (pair + 1.0))[None, None, :]
    return jnp.transpose(summed / damping, (1, 0, 2))[:, None, :, :]


def solution(mesh):
    block = P("fold", None, "lat", "lon")
    in_specs = (block,) * 5 + (P(), P("lon", "lat", None), P("fold"))
    out_specs = P("fold", "lon", "lat", None)
    return jax.shard_map(local, mesh=mesh, in_specs=in_specs, out_specs=out_specs, check_vma=False)
```

time: 421 us -> 196 us (0.47)
  Pallas kernels: 276 us -> 94.4 us
  waiting for transfers between devices: 64.8 us -> 13.3 us
  local copies, waits for them, and re-layouts: 37.2 us -> 53 us
  between operations: 13.6 us -> 0.26 us
  starting transfers between devices: 11.4 us -> 20.6 us
    pallas_call x1, Pallas kernels: 276 us -> 94.4 us  [interpolated_waves(): pl.pallas_call(functools.partial(interp_kernel, margin), grid=(levels,),...]
    unnamed x3 -> x0, waiting for transfers between devices: 34.8 us -> none
    reduce_scatter x1 -> x0, waiting for transfers between devices: 27 us -> none  [local(): coeffs = lax.psum_scatter(by_slot, 'lon', scatter_dimension=0, tiled=True)]
    unnamed x15 -> x17, local copies, waits for them, and re-layouts: 0.68 us -> 18.2 us
    ppermute x5 -> x11, waiting for transfers between devices: 1.87 us -> 12.2 us  [the longest x6 10.7 us: scatter_sum(): lax.ppermute(piece, axis, [(i, (i + step) % count) for i in range(count)])]
    ppermute x5 -> x11, starting transfers between devices: 11.3 us -> 20.5 us  [the longest x6 9.22 us: scatter_sum(): lax.ppermute(piece, axis, [(i, (i + step) % count) for i in range(count)])]
    ppermute x2 -> x0, local copies, waits for them, and re-layouts: 4.6 us -> none  [the longest x1 2.31 us: halos_of(): lax.ppermute(edge(0, margin), 'lon', [((i + 1) % n_lon, i) for i in range...]
    slice x10 -> x7, local copies, waits for them, and re-layouts: 18.2 us -> 20.4 us  [the longest x3 14.2 us: halos_of(): head, tail = (grid[:, :HEAD], grid[:, rows - HEAD:])]
  transfers between devices with their start and end apart: 8 -> 12, of which waited for: 4 -> 7; matrix products, arithmetic and copies ran while one was open for 6% -> 14% of each run, Pallas kernels for 0% -> 0%
where the time goes in v2:
time: 196 us; the launch traced here: 195 us
  Pallas kernels  94.4 us (48%)
  local copies, waits for them, and re-layouts  53 us (27%)
  starting transfers between devices  20.6 us (11%)
  waiting for transfers between devices  13.3 us (7%)
  other arithmetic  11.5 us (6%)
    pallas_call x1, Pallas kernels, interpolated_waves(): pl.pallas_call(functools.partial(interp_kernel, margin), grid=(levels,),...  94.4 us
    unnamed x17, local copies, waits for them, and re-layouts  18.2 us
    slice x3, local copies, waits for them, and re-layouts, halos_of(): head, tail = (grid[:, :HEAD], grid[:, rows - HEAD:])  14.2 us
    ppermute x6, waiting for transfers between devices, scatter_sum(): lax.ppermute(piece, axis, [(i, (i + step) % count) for i in range(count)])  10.7 us
    ppermute x6, starting transfers between devices, scatter_sum(): lax.ppermute(piece, axis, [(i, (i + step) % count) for i in range(count)])  9.22 us
    ppermute x1, starting transfers between devices, halos_of(): north = lax.ppermute(tail, 'lat', [(i, i + 1) for i in range(last)])  5.64 us
  transfers between devices with their start and end apart: 12, of which 7 were waited for; matrix products, arithmetic and copies ran while one was open for 14% of the time, Pallas kernels for 0%

profile of v2, /device:TPU:0, one launch (start us, length us, event | category | flops | bytes accessed | tf_op | source)
XLA Modules:
  0.0 195.0 jit_solution(3154395180186357689)
XLA Ops:
  0.0 8.0 %copy.45 = f32[1,12,160,640]{2,3,1,0:T(8,128)} copy(f32[1,12,160,640]{3,2,1,0:T(8,128)} %param.8) | data formatting | bytes 9830400 | tf_op args[0]
  8.0 7.6 %fusion.23 = (f32[12,8,640]{1,2,0:T(8,128)}, f32[12,8,640]{1,2,0:T(8,128)}) fusion(f32[12,160,640]{1,2,0:T(8,128)} %bitcast.63), kind=kLoop, calls=%fused_computation.51 | loop fusion | bytes 983040 | tf_op jit(solution)/shard_map/slice | solution.py:189
  15.5 3.3 %copy.46 = f32[12,8,640]{2,1,0:T(8,128)} copy(f32[12,8,640]{1,2,0:T(8,128)} %get-tuple-element.8) | data formatting | bytes 491520 | tf_op jit(solution)/shard_map/slice | solution.py:189
  18.9 5.6 %collective-permute-start = (f32[12,8,640]{2,1,0:T(8,128)}, f32[12,8,640]{2,1,0:T(8,128)}, u32[]{:S(2)}, u32[]{:S(2)}) collective-permute-start(f32[12,8,640]{2,1,0:T(8,128)} %copy.46), channel_id=1, source_target_pairs={{0,8},{8,16},{16,24},{1,9},{9,17},{17,25},{2,10},{10,18},{18,26},{... | collective-permute-start | bytes 737288 | tf_op jit(solution)/shard_map/ppermute | solution.py:190
  25.9 3.3 %copy.47 = f32[12,8,640]{2,1,0:T(8,128)} copy(f32[12,8,640]{1,2,0:T(8,128)} %get-tuple-element.7) | data formatting | bytes 491520 | tf_op jit(solution)/shard_map/slice | solution.py:189
  33.4 1.8 subtract_convert_fusion
  35.2 1.6 fusion.22
  37.8 1.5 fusion.27
  40.8 1.5 rev.6
  42.3 1.5 fusion.26
  45.4 1.5 fusion.25
  49.2 1.7 maximum_bitcast_fusion.3
  61.5 1.7 maximum_bitcast_fusion.table
  65.3 94.4 %shard_map.82 = f32[12,4,8,160]{3,2,1,0:T(8,128)} custom-call(s32[1]{0:T(128)} %bitcast.2.last, f32[12,160,640]{2,1,0:T(8,128)} %bitcast.65, f32[12,8,640]{2,1,0:T(8,128)} %collective-permute-done.north, f32[12,8,640]{2,1,0:T(8,128)} %collective-permute-done.1.below, f32[12,8,640]{2,1,0:T(8,128)} %collective-permute-done.2.mirror, ...), custom_call_target="tpu_custom_call" | custom-call | tf_op jit(solution)/shard_map/pallas_call | solution.py:155
  159.7 1.7 dynamic-slice_bitcast_fusion.2
  161.4 2.3 %collective-permute-start.7 = (f32[12,8,160]{2,1,0:T(8,128)}, f32[12,8,160]{2,1,0:T(8,128)S(1)}, u32[]{:S(2)}, u32[]{:S(2)}) collective-permute-start(f32[12,8,160]{2,1,0:T(8,128)} %get-tuple-element.12), channel_id=1, source_target_pairs={{0,6},{2,0},{4,2},{6,4},{1,7},{3,1},{5,3},{7,5},{8,14},{10,8},{12,... | collective-permute-start | bytes 184328 | tf_op jit(solution)/shard_map/ppermute | solution.py:213
  163.7 1.5 collective-permute-start.6
  165.4 2.2 %collective-permute-done.7 = f32[12,8,160]{2,1,0:T(8,128)S(1)} collective-permute-done((f32[12,8,160]{2,1,0:T(8,128)}, f32[12,8,160]{2,1,0:T(8,128)S(1)}, u32[]{:S(2)}, u32[]{:S(2)}) %collective-permute-start.7) | collective-permute-done | bytes 61472 | tf_op jit(solution)/shard_map/ppermute | solution.py:213
  173.5 1.9 fusion.2
  178.2 1.8 copy.63
  180.0 1.9 squeeze.57
  183.2 4.7 %collective-permute-start.11 = (f32[1,6,2560]{2,0,1:T(1,128)S(1)}, f32[1,6,2560]{2,0,1:T(1,128)S(1)}, u32[]{:S(2)}, u32[]{:S(2)}) collective-permute-start(f32[1,6,2560]{2,0,1:T(1,128)S(1)} %get-tuple-element.15), channel_id=1, source_target_pairs={{0,24},{8,0},{16,8},{24,16},{1,25},{9,1},{17,9},{25,17},{2,26},{10... | collective-permute-start | bytes 184328 | tf_op jit(solution)/shard_map/ppermute | solution.py:213
  188.5 1.8 collective-permute-done.11
  190.3 3.8 %collective-permute-done.10 = f32[1,6,2560]{2,0,1:T(1,128)S(1)} collective-permute-done((f32[1,6,2560]{2,0,1:T(1,128)S(1)}, f32[1,6,2560]{2,0,1:T(1,128)S(1)}, u32[]{:S(2)}, u32[]{:S(2)}) %collective-permute-start.10) | collective-permute-done | bytes 61472 | tf_op jit(solution)/shard_map/ppermute | solution.py:213
  (63 shorter events, 35.9 us)
Async XLA Ops:
  0.0 173.5 %copy-start = (f32[4,160,1280]{2,1,0:T(8,128)S(1)}, f32[4,160,1280]{2,1,0:T(8,128)}, u32[]{:S(2)}) copy-start(f32[4,160,1280]{2,1,0:T(8,128)} %param.14) | copy-start | bytes 9830404
  15.5 15.0 %copy-start.3 = (s32[16]{0:T(128)S(1)}, s32[16]{0:T(128)}, u32[]{:S(2)}) copy-start(s32[16]{0:T(128)} %param.13) | copy-start | bytes 196
  18.9 26.5 %collective-permute-start = (f32[12,8,640]{2,1,0:T(8,128)}, f32[12,8,640]{2,1,0:T(8,128)}, u32[]{:S(2)}, u32[]{:S(2)}) collective-permute-start(f32[12,8,640]{2,1,0:T(8,128)} %copy.46), channel_id=1, source_target_pairs={{0,8},{8,16},{16,24},{1,9},{9,17},{17,25},{2,10},{10,18},{18,26},{... | collective-permute-start | bytes 737288 | tf_op jit(solution)/shard_map/ppermute | solution.py:190
  24.5 13.3 %collective-permute-start.2 = (f32[12,8,640]{2,1,0:T(8,128)}, f32[12,8,640]{2,1,0:T(8,128)}, u32[]{:S(2)}, u32[]{:S(2)}) collective-permute-start(f32[12,8,640]{2,1,0:T(8,128)} %copy.46), channel_id=1, source_target_pairs={{24,25},{25,24},{26,27},{27,26},{28,29},{29,28},{30,31},{31,30}} | collective-permute-start | bytes 737288 | tf_op jit(solution)/shard_map/ppermute | solution.py:193
  29.2 13.1 %collective-permute-start.1 = (f32[12,8,640]{2,1,0:T(8,128)}, f32[12,8,640]{2,1,0:T(8,128)}, u32[]{:S(2)}, u32[]{:S(2)}) collective-permute-start(f32[12,8,640]{2,1,0:T(8,128)} %copy.47), channel_id=1, source_target_pairs={{8,0},{16,8},{24,16},{9,1},{17,9},{25,17},{10,2},{18,10},{26,18},{... | collective-permute-start | bytes 737288 | tf_op jit(solution)/shard_map/ppermute | solution.py:191
  50.8 12.4 %collective-permute-start.3 = (f32[12,8,176]{2,1,0:T(8,128)}, f32[12,8,176]{2,1,0:T(8,128)}, u32[]{:S(2)}, u32[]{:S(2)}) collective-permute-start(f32[12,8,176]{2,1,0:T(8,128)} %maximum_bitcast_fusion.3), channel_id=1, source_target_pairs={{0,2},{2,4},{4,6},{6,0},{1,3},{3,5},{5,7},{7,1},{8,10},{10,12},{12... | collective-permute-start | bytes 202760 | tf_op jit(solution)/shard_map/ppermute | solution.py:201
  60.0 4.7 %collective-permute-start.4 = (f32[12,8,176]{2,1,0:T(8,128)S(1)}, f32[12,8,176]{2,1,0:T(8,128)S(1)}, u32[]{:S(2)}, u32[]{:S(2)}) collective-permute-start(f32[12,8,176]{2,1,0:T(8,128)S(1)} %maximum_bitcast_fusion.4), channel_id=1, source_target_pairs={{2,0},{4,2},{6,4},{0,6},{3,1},{5,3},{7,5},{1,7},{10,8},{12,10},{14... | collective-permute-start | bytes 202760 | tf_op jit(solution)/shard_map/ppermute | solution.py:202
  64.7 0.6 copy-start.1
  161.4 6.2 %collective-permute-start.7 = (f32[12,8,160]{2,1,0:T(8,128)}, f32[12,8,160]{2,1,0:T(8,128)S(1)}, u32[]{:S(2)}, u32[]{:S(2)}) collective-permute-start(f32[12,8,160]{2,1,0:T(8,128)} %get-tuple-element.12), channel_id=1, source_target_pairs={{0,6},{2,0},{4,2},{6,4},{1,7},{3,1},{5,3},{7,5},{8,14},{10,8},{12,... | collective-permute-start | bytes 184328 | tf_op jit(solution)/shard_map/ppermute | solution.py:213
  163.7 5.4 %collective-permute-start.6 = (f32[12,8,160]{2,1,0:T(8,128)}, f32[12,8,160]{2,1,0:T(8,128)S(1)}, u32[]{:S(2)}, u32[]{:S(2)}) collective-permute-start(f32[12,8,160]{2,1,0:T(8,128)} %get-tuple-element.13), channel_id=1, source_target_pairs={{0,4},{2,6},{4,0},{6,2},{1,5},{3,7},{5,1},{7,3},{8,12},{10,14},{12... | collective-permute-start | bytes 184328 | tf_op jit(solution)/shard_map/ppermute | solution.py:213
  165.3 5.8 %collective-permute-start.5 = (f32[12,8,160]{2,1,0:T(8,128)}, f32[12,8,160]{2,1,0:T(8,128)}, u32[]{:S(2)}, u32[]{:S(2)}) collective-permute-start(f32[12,8,160]{2,1,0:T(8,128)} %get-tuple-element.11), channel_id=1, source_target_pairs={{0,2},{2,4},{4,6},{6,0},{1,3},{3,5},{5,7},{7,1},{8,10},{10,12},{12... | collective-permute-start | bytes 184328 | tf_op jit(solution)/shard_map/ppermute | solution.py:213
  169.1 0.6 copy-start.2
  172.1 1.3 collective-permute-start.8
  173.5 20.7 %copy-start.4 = (f32[6]{0:T(128)S(1)}, f32[6]{0:T(128)}, u32[]{:S(2)}) copy-start(f32[6]{0:T(128)} %param.15) | copy-start | bytes 76
  183.2 7.2 %collective-permute-start.11 = (f32[1,6,2560]{2,0,1:T(1,128)S(1)}, f32[1,6,2560]{2,0,1:T(1,128)S(1)}, u32[]{:S(2)}, u32[]{:S(2)}) collective-permute-start(f32[1,6,2560]{2,0,1:T(1,128)S(1)} %get-tuple-element.15), channel_id=1, source_target_pairs={{0,24},{8,0},{16,8},{24,16},{1,25},{9,1},{17,9},{25,17},{2,26},{10... | collective-permute-start | bytes 184328 | tf_op jit(solution)/shard_map/ppermute | solution.py:213
  187.9 6.3 %collective-permute-start.10 = (f32[1,6,2560]{2,0,1:T(1,128)S(1)}, f32[1,6,2560]{2,0,1:T(1,128)S(1)}, u32[]{:S(2)}, u32[]{:S(2)}) collective-permute-start(f32[1,6,2560]{2,0,1:T(1,128)S(1)} %get-tuple-element.16), channel_id=1, source_target_pairs={{0,16},{8,24},{16,0},{24,8},{1,17},{9,25},{17,1},{25,9},{2,18},{10... | collective-permute-start | bytes 184328 | tf_op jit(solution)/shard_map/ppermute | solution.py:213
  187.9 6.3 %collective-permute-start.9 = (f32[1,6,2560]{2,0,1:T(1,128)S(1)}, f32[1,6,2560]{2,0,1:T(1,128)S(1)}, u32[]{:S(2)}, u32[]{:S(2)}) collective-permute-start(f32[1,6,2560]{2,0,1:T(1,128)S(1)} %get-tuple-element.14), channel_id=1, source_target_pairs={{0,8},{8,16},{16,24},{24,0},{1,9},{9,17},{17,25},{25,1},{2,10},{10... | collective-permute-start | bytes 184328 | tf_op jit(solution)/shard_map/ppermute | solution.py:213
